TPU v7x, 32 devices: a whole 2x2x4 slice. The times are simulated.
32 devices in a mesh: grp: 4 (over y, x), tp: 8 (over z, core).
Axes of the slice: x: 2, y: 2, z: 4, core: 2. Of those that a mesh axis runs over, the one named last changes fastest.
Arguments:
- key_cache: bfloat16 [4, 8, 768, 512], P('grp', 'tp'), may hold values from -6 to 6
- value_cache: bfloat16 [4, 8, 768, 512], P('grp', 'tp'), may hold values from -12 to 12
- lengths: int32 [4, 8], P('grp', 'tp'), may hold values from 256 to 768, as said below
- queries: bfloat16 [4, 1, 8, 8192], P('grp', None, 'tp'), may hold values from -12 to 12
- new_keys: bfloat16 [4, 1, 8, 512], P('grp', None, 'tp'), may hold values from -18 to 18
- new_values: bfloat16 [4, 1, 8, 512], P('grp', None, 'tp'), may hold values from -12 to 12
- residual: bfloat16 [4, 1, 8, 8192], P('grp', None, 'tp'), may hold values from -4 to 4
- norm_gain: float32 [8192], replicated, may hold values from 0.25 to 1.75
- gate_weight: bfloat16 [4, 13312, 8192], P('grp', 'tp'), may hold values from -0.0625 to 0.0625
- up_weight: bfloat16 [4, 13312, 8192], P('grp', 'tp'), may hold values from -0.0625 to 0.0625
- down_weight: bfloat16 [4, 13312, 8192], P('grp', 'tp'), may hold values from -0.0390625 to 0.0390625
Outputs:
- mixed: bfloat16 [4, 1, 8, 8192], P('grp', None, 'tp')
Inputs may be any that keep to these rules, and one draw needn't show every extreme that they name: `lengths`: some row has exactly 768 valid positions.
All inputs are finite; a program needn't handle non-finite values.
Results may differ from a plain program's by a relative error of at most 0.005.
Values may be sent and summed in bfloat16 or wider, within the bound.
A program may use at most 128 MiB of HBM per device.

v0:
```python
import jax
import jax.numpy as jnp
from jax import lax
from jax.sharding import PartitionSpec as P

HEADS = 64
HD = 128
KVH = 4
masked_score = -1e30


def feed_rows(normed_rows, gate_weight, up_weight, down_weight):
    numbers = (((1,), (1,)), ((), ()))
    gate_part = lax.dot_general(
        normed_rows, gate_weight[0], numbers, preferred_element_type=jnp.float32
    )
    up_part = lax.dot_general(
        normed_rows, up_weight[0], numbers, preferred_element_type=jnp.float32
    )
    product = (jax.nn.silu(gate_part) * up_part).astype(jnp.bfloat16)
    return jnp.dot(product, down_weight[0], preferred_element_type=jnp.float32)


def local(
    key_cache,
    value_cache,
    lengths,
    queries,
    new_keys,
    new_values,
    residual,
    norm_gain,
    gate_weight,
    up_weight,
    down_weight,
):
    groups = lax.axis_size("grp")
    members = lax.axis_size("tp")
    serving = lax.axis_index("grp") < groups // 2
    step_count = queries.shape[1]
    own_rows = queries.shape[2]
    model_width = queries.shape[3]
    head_share = HEADS // KVH
    slot_count = key_cache.shape[2]
    score_scale = HD ** (-0.5)
    own_heads = queries[0].reshape(step_count, own_rows, KVH, head_share, HD)
    cache_keys = key_cache[0].reshape(own_rows, slot_count, KVH, HD)
    cache_values = value_cache[0].reshape(own_rows, slot_count, KVH, HD)
    positions = jnp.arange(slot_count)
    usable = positions[None, :] < lengths[0][:, None]
    usable_mask = usable[None, :, None, None, :]
    cache_scores = (
        jnp.einsum("srjgd,rpjd->srjgp", own_heads, cache_keys, preferred_element_type=jnp.float32)
        * score_scale
    )
    cache_scores = jnp.where(usable_mask, cache_scores, masked_score)
    fresh_keys = new_keys[0].reshape(step_count, own_rows, KVH, HD)
    fresh_values = new_values[0].reshape(step_count, own_rows, KVH, HD)
    fresh_scores = (
        jnp.einsum("srjgd,trjd->srjgt", own_heads, fresh_keys, preferred_element_type=jnp.float32)
        * score_scale
    )
    causal = jnp.arange(step_count)[:, None] >= jnp.arange(step_count)[None, :]
    causal_mask = causal[:, None, None, None, :]
    fresh_scores = jnp.where(causal_mask, fresh_scores, masked_score)
    ceiling = jnp.maximum(jnp.max(cache_scores, axis=-1), jnp.max(fresh_scores, axis=-1))
    cache_exp = jnp.where(usable_mask, jnp.exp(cache_scores - ceiling[..., None]), 0.0)
    fresh_exp = jnp.where(causal_mask, jnp.exp(fresh_scores - ceiling[..., None]), 0.0)
    denominator = jnp.sum(cache_exp, axis=-1) + jnp.sum(fresh_exp, axis=-1)
    cache_weighted = jnp.einsum(
        "srjgp,rpjd->srjgd",
        cache_exp.astype(jnp.bfloat16),
        cache_values,
        preferred_element_type=jnp.float32,
    )
    fresh_weighted = jnp.einsum(
        "srjgt,trjd->srjgd",
        fresh_exp.astype(jnp.bfloat16),
        fresh_values,
        preferred_element_type=jnp.float32,
    )
    attended = (cache_weighted + fresh_weighted) / denominator[..., None]
    attended = attended.reshape(step_count, own_rows, model_width)
    hidden = residual[0].astype(jnp.float32) + attended
    spread_sq = jnp.mean(hidden * hidden, axis=-1, keepdims=True)
    normed = (hidden * lax.rsqrt(spread_sq + 1e-05) * norm_gain).astype(jnp.bfloat16)
    block_rows = step_count * own_rows
    flat_rows = normed.reshape(block_rows, model_width)
    ffn_first = groups // 2
    group_block = lax.all_gather(flat_rows, "tp", axis=0, tiled=True).reshape(
        members, block_rows, model_width
    )
    all_rows = lax.all_gather(group_block, "grp", axis=1, tiled=True)
    real_rows = all_rows[:, : ffn_first * block_rows].reshape(
        members * ffn_first * block_rows, model_width
    )
    within = lax.psum_scatter(
        lax.cond(
            serving,
            lambda operand: jnp.zeros(
                (ffn_first * block_rows * lax.axis_size("tp"), model_width), jnp.float32
            ),
            lambda operand: feed_rows(operand, gate_weight, up_weight, down_weight),
            real_rows,
        ),
        "tp",
        scatter_dimension=0,
        tiled=True,
    )
    padded = jnp.concatenate(
        [within, jnp.zeros(((groups - ffn_first) * block_rows, model_width), jnp.float32)], 0
    )
    summed = lax.psum_scatter(padded, "grp", scatter_dimension=0, tiled=True)
    mixed = (hidden + summed.reshape(step_count, own_rows, model_width)).astype(jnp.bfloat16)
    mixed = jnp.where(serving, mixed, jnp.zeros_like(mixed))
    return mixed[None]


def solution(mesh):
    return jax.shard_map(
        local,
        mesh=mesh,
        in_specs=(
            P("grp", "tp", None, None),
            P("grp", "tp", None, None),
            P("grp", "tp"),
            P("grp", None, "tp", None),
            P("grp", None, "tp", None),
            P("grp", None, "tp", None),
            P("grp", None, "tp", None),
            P(),
            P("grp", "tp", None),
            P("grp", "tp", None),
            P("grp", "tp", None),
        ),
        out_specs=P("grp", None, "tp", None),
        check_vma=False,
    )
```

profile of v0, /device:TPU:0, one launch (start us, length us, event | category | flops | bytes accessed | tf_op | source)
XLA Modules:
  0.0 188.5 jit_solution(14599634890557836540)
XLA Ops:
  7.2 1.8 reshape.145
  9.0 0.1 reduce.4
  9.1 0.8 fusion.38
  9.9 0.4 fusion.42
  10.3 0.2 fusion.28
  10.5 0.8 convert_element_type.47
  11.3 1.8 reshape.149
  13.1 0.7 convert.12
  13.8 0.9 fusion.37
  15.3 0.8 multiply_convert_fusion
  16.1 15.7 %all-gather = bf16[65536]{0:T(1024)(128)(2,1)S(1)} all-gather(bf16[8192]{0:T(1024)(128)(2,1)S(1)} %multiply_convert_fusion), channel_id=2, replica_groups=mesh['grp'=4,'tp'=8] {'tp'}, dimensions={0}, use_global_device_ids=true | all-gather | bytes 147456 | tf_op jit(solution)/shard_map/all_gather | solution.py:90
  31.8 0.1 reshape.161
  31.9 10.3 %all-gather.1 = bf16[8,32768]{1,0:T(8,128)(2,1)S(1)} all-gather(bf16[8,8192]{1,0:T(8,128)(2,1)S(1)} %reshape.161), channel_id=3, replica_groups=mesh['grp'=4,'tp'=8] {'grp'}, dimensions={1}, use_global_device_ids=true | all-gather | bytes 655360 | tf_op jit(solution)/shard_map/all_gather | solution.py:93
  42.2 0.4 reshape.162
  42.7 0.1 conditional.1
  42.7 0.8 copy-done.2
  43.6 0.0 all-reduce.8.cloned.1.call-start
  43.6 0.6 dynamic-slice
  44.9 90.4 %all-reduce.6.cloned.1.call-done = f32[16,8192]{1,0:T(8,128)} async-done(((f32[16,8192]{1,0:T(8,128)}), f32[16,8192]{1,0:T(8,128)}) %all-reduce.6.cloned.1.call-update) | async-done | bytes 524304
  135.3 1.0 constant_dynamic-slice_fusion
  136.3 0.7 concatenate.3
  137.0 0.6 dynamic-slice.2
  137.6 41.8 %all-reduce.8.cloned.1.call-done = f32[4,8192]{1,0:T(4,128)} async-done(((f32[4,8192]{1,0:T(4,128)}), f32[4,8192]{1,0:T(4,128)}) %all-reduce.8.cloned.1.call-update) | async-done | bytes 131088
  179.5 2.2 %broadcast_select_fusion = bf16[1,1,1,8192]{3,2,1,0:T(2,128)(2,1)} fusion(pred[]{:T(512)S(6)} %lt.19, f32[4,8192]{1,0:T(4,128)} %all-reduce.8.cloned.1.call-done, u32[]{:T(128)} %bitcast.23, f32[1,1,1,8192]{3,2,1,0:T(1,128)S(1)} %bitcast.74, bf16[1,1,1,8192]{3,2,1,0:T(2,128)(2,1)S(1)} %copy-done.3), kind=kLoop, calls=%fused_computation.31 | loop fusion | flops 40960 | bytes 98309 | tf_op jit(solution)/shard_map/jit(_where)/select_n | solution.py:115
  (18 shorter events, 0.1 us)
Async XLA Ops:
  6.5 2.4 %copy-start = (bf16[1,1,1,8192]{3,2,1,0:T(2,128)(2,1)S(1)}, bf16[1,1,1,8192]{3,2,1,0:T(2,128)(2,1)}, u32[]{:S(2)}) copy-start(bf16[1,1,1,8192]{3,2,1,0:T(2,128)(2,1)} %param.16) | copy-start | bytes 49156
  6.5 128.8 %all-reduce.6.cloned.1.call-start = ((), (), s32[]{:S(2)}) async-start(), calls=%async_computation | async-start | bytes 1048576
  42.6 1.0 copy-start.5
  42.6 94.4 %copy-start.4 = (u32[32]{0:T(128)S(1)}, u32[32]{0:T(128)}, u32[]{:S(2)}) copy-start(u32[32]{0:T(128)} %constant.51) | copy-start | bytes 388
  42.6 136.8 %copy-start.3 = (bf16[1,1,1,8192]{3,2,1,0:T(2,128)(2,1)S(1)}, bf16[1,1,1,8192]{3,2,1,0:T(2,128)(2,1)}, u32[]{:S(2)}) copy-start(bf16[1,1,1,8192]{3,2,1,0:T(2,128)(2,1)} %param.19) | copy-start | bytes 49156
  42.7 0.8 copy-start.2
  42.7 139.0 %copy-start.1 = (bf16[1,1,1,8192]{3,2,1,0:T(2,128)(2,1)S(1)}, bf16[1,1,1,8192]{3,2,1,0:T(2,128)(2,1)}, u32[]{:S(2)}) copy-start(bf16[1,1,1,8192]{3,2,1,0:T(2,128)(2,1)} %param.16) | copy-start | bytes 49156
  43.6 135.9 %all-reduce.8.cloned.1.call-start = ((), (), s32[]{:S(2)}) async-start(), calls=%async_computation.1 | async-start | bytes 262144
Sparse Core Ops, SparseCore 0:
  43.7 91.5 all-reduce.5
  138.2 41.2 all-reduce.7
where the time goes:
time: 189 us
  waiting for transfers between devices  132 us (70%)
  blocking collectives  26 us (14%)
  between operations  15.5 us (8%)
  local copies, waits for them, and re-layouts  7.69 us (4%)
  other arithmetic  4.78 us (3%)
  matrix products  2.09 us (1%)
    unnamed x4, waiting for transfers between devices  132 us
    all_gather x1, blocking collectives, local(): lax.all_gather(flat_rows, 'tp', axis=0, tiled=True)  15.7 us
    all_gather x1, blocking collectives, local(): all_rows = lax.all_gather(group_block, 'grp', axis=1, tiled=True)  10.3 us
  transfers between devices with their start and end apart: 2, of which 2 were waited for; matrix products, arithmetic and copies ran while one was open for 1% of the time, Pallas kernels for 0%

commit v1 on v0

--- a/solution.py
+++ b/solution.py
@@ -1,3 +1,4 @@
+import functools
 import jax
 import jax.numpy as jnp
 from jax import lax
@@ -7,6 +8,16 @@
 HD = 128
 KVH = 4
 masked_score = -1e30
+
+
+def _build_rates(q_in, axis_tag):
+    extent = lax.axis_size(axis_tag)
+    parts_out = jnp.tile(q_in, list(map(lambda p: extent if p == 0 else 1, range(q_in.ndim))))
+    x_now = lax.all_to_all(parts_out, axis_tag, split_axis=0, concat_axis=0, tiled=True)
+    return x_now
+
+
+search_islands_on = functools.partial(_build_rates, axis_tag="tp")
 
 
 def feed_rows(normed_rows, gate_weight, up_weight, down_weight):
@@ -87,9 +98,7 @@
     block_rows = step_count * own_rows
     flat_rows = normed.reshape(block_rows, model_width)
     ffn_first = groups // 2
-    group_block = lax.all_gather(flat_rows, "tp", axis=0, tiled=True).reshape(
-        members, block_rows, model_width
-    )
+    group_block = search_islands_on(flat_rows).reshape(members, block_rows, model_width)
     all_rows = lax.all_gather(group_block, "grp", axis=1, tiled=True)
     real_rows = all_rows[:, : ffn_first * block_rows].reshape(
         members * ffn_first * block_rows, model_width

time: 189 us -> 187 us (0.989)
  blocking collectives: 26 us -> 10 us
  starting transfers between devices: 0.04 us -> 6.43 us
  waiting for transfers between devices: 132 us -> 138 us
    all_gather x1 -> x0, blocking collectives: 15.7 us -> none  [local(): lax.all_gather(flat_rows, 'tp', axis=0, tiled=True)]
    all_to_all x0 -> x1, waiting for transfers between devices: none -> 6.7 us  [_build_rates(): lax.all_to_all(parts_out, axis_tag, split_axis=0, concat_axis=0, tiled=True)]
    all_to_all x0 -> x1, starting transfers between devices: none -> 6.35 us  [_build_rates(): lax.all_to_all(parts_out, axis_tag, split_axis=0, concat_axis=0, tiled=True)]
    unnamed x15 -> x17, local copies, waits for them, and re-layouts: 3.03 us -> 3.86 us
    another operation x3 -> x5, local copies, waits for them, and re-layouts: 3.54 us -> 4.19 us
  transfers between devices with their start and end apart: 2 -> 3, of which waited for: 2 -> 3; matrix products, arithmetic and copies ran while one was open for 1% -> 1% of each run, Pallas kernels for 0% -> 0%
where the time goes in v1:
time: 187 us
  waiting for transfers between devices  138 us (74%)
  between operations  15.6 us (8%)
  blocking collectives  10 us (5%)
  local copies, waits for them, and re-layouts  8.87 us (5%)
  starting transfers between devices  6.43 us (3%)
  other arithmetic  6.19 us (3%)
  matrix products  2.09 us (1%)
    unnamed x4, waiting for transfers between devices  131 us
    all_gather x1, blocking collectives, local(): all_rows = lax.all_gather(group_block, 'grp', axis=1, tiled=True)  10 us
    all_to_all x1, waiting for transfers between devices, _build_rates(): lax.all_to_all(parts_out, axis_tag, split_axis=0, concat_axis=0, tiled=True)  6.7 us
    all_to_all x1, starting transfers between devices, _build_rates(): lax.all_to_all(parts_out, axis_tag, split_axis=0, concat_axis=0, tiled=True)  6.35 us
    unnamed x17, local copies, waits for them, and re-layouts  3.86 us
  transfers between devices with their start and end apart: 3, of which 3 were waited for; matrix products, arithmetic and copies ran while one was open for 1% of the time, Pallas kernels for 0%

profile of v1, /device:TPU:0, one launch (start us, length us, event | category | flops | bytes accessed | tf_op | source)
XLA Modules:
  0.0 186.9 jit_solution(13162828479628622460)
XLA Ops:
  7.2 1.8 reshape.149
  9.1 0.8 fusion.38
  9.9 0.4 fusion.42
  10.3 0.2 fusion.28
  10.5 0.8 convert_element_type.47
  11.3 1.8 reshape.153
  13.1 0.7 convert.12
  13.7 0.9 fusion.37
  15.3 0.8 multiply_convert_fusion
  16.2 0.5 broadcast.50
  16.8 1.4 reduce.5
  18.2 0.7 reshape.169
  18.9 6.4 %all-to-all-start = ((bf16[8,2,4096]{2,1,0:T(2,128)(2,1)}), bf16[8,2,4096]{2,1,0:T(2,128)(2,1)S(1)}, u32[]{:S(2)}, u32[]{:S(2)}) async-start(bf16[8,2,4096]{2,1,0:T(2,128)(2,1)} %reshape.169), calls=%async_computation | async-start | bytes 262144 | tf_op jit(solution)/shard_map/all_to_all | solution.py:16
  25.3 6.7 %all-to-all-done = bf16[8,2,4096]{2,1,0:T(2,128)(2,1)S(1)} async-done(((bf16[8,2,4096]{2,1,0:T(2,128)(2,1)}), bf16[8,2,4096]{2,1,0:T(2,128)(2,1)S(1)}, u32[]{:S(2)}, u32[]{:S(2)}) %all-to-all-start) | async-done | bytes 131104 | tf_op jit(solution)/shard_map/all_to_all | solution.py:16
  32.1 0.2 copy.22
  32.3 10.0 %all_gather.3 = bf16[8,4,8192]{2,0,1:T(8,128)(2,1)S(1)} all-gather(bf16[8,1,8192]{2,0,1:T(8,128)(2,1)S(1)} %copy.22), channel_id=1, replica_groups=mesh['grp'=4,'tp'=8] {'grp'}, dimensions={1}, use_global_device_ids=true | all-gather | bytes 655360 | tf_op jit(solution)/shard_map/all_gather | solution.py:102
  42.4 0.8 copy-done.2
  43.3 0.6 dynamic-slice
  44.5 89.1 %all-reduce.6.cloned.1.call-done = f32[16,8192]{1,0:T(8,128)} async-done(((f32[16,8192]{1,0:T(8,128)}), f32[16,8192]{1,0:T(8,128)}) %all-reduce.6.cloned.1.call-update) | async-done | bytes 524304
  133.7 1.0 constant_dynamic-slice_fusion
  134.6 0.7 concatenate.3
  135.4 0.6 dynamic-slice.2
  136.0 41.8 %all-reduce.8.cloned.1.call-done = f32[4,8192]{1,0:T(4,128)} async-done(((f32[4,8192]{1,0:T(4,128)}), f32[4,8192]{1,0:T(4,128)}) %all-reduce.8.cloned.1.call-update) | async-done | bytes 131088
  177.8 2.2 %broadcast_select_fusion = bf16[1,1,1,8192]{3,2,1,0:T(2,128)(2,1)} fusion(pred[]{:T(512)S(6)} %lt.19, f32[4,8192]{1,0:T(4,128)} %all-reduce.8.cloned.1.call-done, u32[]{:T(128)} %bitcast.23, f32[1,1,1,8192]{3,2,1,0:T(1,128)S(1)} %bitcast.74, bf16[1,1,1,8192]{3,2,1,0:T(2,128)(2,1)S(1)} %copy-done.3), kind=kLoop, calls=%fused_computation.31 | loop fusion | flops 40960 | bytes 98309 | tf_op jit(solution)/shard_map/jit(_where)/select_n | solution.py:124
  (23 shorter events, 0.6 us)
Async XLA Ops:
  6.5 2.4 %copy-start = (bf16[1,1,1,8192]{3,2,1,0:T(2,128)(2,1)S(1)}, bf16[1,1,1,8192]{3,2,1,0:T(2,128)(2,1)}, u32[]{:S(2)}) copy-start(bf16[1,1,1,8192]{3,2,1,0:T(2,128)(2,1)} %param.16) | copy-start | bytes 49156
  18.9 13.1 %all-to-all-start = ((bf16[8,2,4096]{2,1,0:T(2,128)(2,1)}), bf16[8,2,4096]{2,1,0:T(2,128)(2,1)S(1)}, u32[]{:S(2)}, u32[]{:S(2)}) async-start(bf16[8,2,4096]{2,1,0:T(2,128)(2,1)} %reshape.169), calls=%async_computation | async-start | bytes 262144 | tf_op jit(solution)/shard_map/all_to_all | solution.py:16
  25.2 108.4 %all-reduce.6.cloned.1.call-start = ((), (), s32[]{:S(2)}) async-start(), calls=%async_computation.1 | async-start | bytes 1048576
  42.3 1.0 copy-start.5
  42.3 93.0 %copy-start.4 = (u32[32]{0:T(128)S(1)}, u32[32]{0:T(128)}, u32[]{:S(2)}) copy-start(u32[32]{0:T(128)} %constant.51) | copy-start | bytes 388
  42.3 135.5 %copy-start.3 = (bf16[1,1,1,8192]{3,2,1,0:T(2,128)(2,1)S(1)}, bf16[1,1,1,8192]{3,2,1,0:T(2,128)(2,1)}, u32[]{:S(2)}) copy-start(bf16[1,1,1,8192]{3,2,1,0:T(2,128)(2,1)} %param.19) | copy-start | bytes 49156
  42.4 0.8 copy-start.2
  42.4 137.6 %copy-start.1 = (bf16[1,1,1,8192]{3,2,1,0:T(2,128)(2,1)S(1)}, bf16[1,1,1,8192]{3,2,1,0:T(2,128)(2,1)}, u32[]{:S(2)}) copy-start(bf16[1,1,1,8192]{3,2,1,0:T(2,128)(2,1)} %param.16) | copy-start | bytes 49156
  43.2 134.6 %all-reduce.8.cloned.1.call-start = ((), (), s32[]{:S(2)}) async-start(), calls=%async_computation.2 | async-start | bytes 262144
Sparse Core Ops, SparseCore 0:
  43.4 90.2 all-reduce.5
  136.5 41.2 all-reduce.7

commit v2 on v0

--- a/solution.py
+++ b/solution.py
@@ -90,7 +90,17 @@
     group_block = lax.all_gather(flat_rows, "tp", axis=0, tiled=True).reshape(
         members, block_rows, model_width
     )
-    all_rows = lax.all_gather(group_block, "grp", axis=1, tiled=True)
+    size, here, width = (lax.axis_size("grp"), lax.axis_index("grp"), group_block.shape[1])
+    right = [(i, (i + 1) % size) for i in range(size)]
+    all_rows = jnp.zeros(
+        (*group_block.shape[:1], size * width, *group_block.shape[1 + 1 :]), group_block.dtype
+    )
+    carried = group_block
+    for step in range(size):
+        source = (here - step) % size
+        all_rows = lax.dynamic_update_slice_in_dim(all_rows, carried, source * width, axis=1)
+        if step < size - 1:
+            carried = lax.ppermute(carried, "grp", right)
     real_rows = all_rows[:, : ffn_first * block_rows].reshape(
         members * ffn_first * block_rows, model_width
     )

time: 189 us -> 209 us (1.11)
  waiting for transfers between devices: 132 us -> 160 us
  blocking collectives: 26 us -> 15.7 us
  starting transfers between devices: 0.04 us -> 2.18 us
    ppermute x0 -> x3, waiting for transfers between devices: none -> 16.3 us  [local(): carried = lax.ppermute(carried, 'grp', right)]
    unnamed x4, waiting for transfers between devices: 132 us -> 144 us
    all_gather x1 -> x0, blocking collectives: 10.3 us -> none  [local(): all_rows = lax.all_gather(group_block, 'grp', axis=1, tiled=True)]
    ppermute x0 -> x3, starting transfers between devices: none -> 2.14 us  [local(): carried = lax.ppermute(carried, 'grp', right)]
  transfers between devices with their start and end apart: 2 -> 5, of which waited for: 2 -> 5; matrix products, arithmetic and copies ran while one was open for 1% -> 1% of each run, Pallas kernels for 0% -> 0%
where the time goes in v2:
time: 209 us; the launch traced here: 208 us
  waiting for transfers between devices  160 us (77%)
  blocking collectives  15.7 us (8%)
  between operations  15.5 us (7%)
  local copies, waits for them, and re-layouts  7.28 us (3%)
  other arithmetic  4.85 us (2%)
  starting transfers between devices  2.18 us (1%)
  matrix products  2.09 us (1%)
    unnamed x4, waiting for transfers between devices  144 us
    ppermute x3, waiting for transfers between devices, local(): carried = lax.ppermute(carried, 'grp', right)  16.3 us
    all_gather x1, blocking collectives, local(): lax.all_gather(flat_rows, 'tp', axis=0, tiled=True)  15.7 us
  transfers between devices with their start and end apart: 5, of which 5 were waited for; matrix products, arithmetic and copies ran while one was open for 1% of the time, Pallas kernels for 0%

profile of v2, /device:TPU:0, one launch (start us, length us, event | category | flops | bytes accessed | tf_op | source)
XLA Modules:
  0.0 208.0 jit_solution(15846915504029643104)
XLA Ops:
  7.2 1.8 reshape.145
  9.0 0.1 reduce.4
  9.1 0.8 fusion.38
  9.9 0.4 fusion.42
  10.3 0.2 fusion.28
  10.5 0.8 convert_element_type.47
  11.3 1.8 reshape.149
  13.1 0.7 convert.12
  13.8 0.9 fusion.37
  15.3 0.8 multiply_convert_fusion
  16.1 15.7 %all-gather = bf16[65536]{0:T(1024)(128)(2,1)S(1)} all-gather(bf16[8192]{0:T(1024)(128)(2,1)S(1)} %multiply_convert_fusion), channel_id=2, replica_groups=mesh['grp'=4,'tp'=8] {'tp'}, dimensions={0}, use_global_device_ids=true | all-gather | bytes 147456 | tf_op jit(solution)/shard_map/all_gather | solution.py:90
  31.9 1.5 collective-permute-start
  33.4 5.2 %collective-permute-done = bf16[8,1,8192]{2,0,1:T(8,128)(2,1)S(1)} collective-permute-done((bf16[8,1,8192]{2,0,1:T(8,128)(2,1)S(1)}, bf16[8,1,8192]{2,0,1:T(8,128)(2,1)S(1)}, u32[]{:S(2)}, u32[]{:S(2)}) %collective-permute-start) | collective-permute-done | bytes 131104 | tf_op jit(solution)/shard_map/ppermute | solution.py:103
  38.6 0.6 collective-permute-start.1
  39.2 5.3 %collective-permute-done.1 = bf16[8,1,8192]{2,0,1:T(8,128)(2,1)S(1)} collective-permute-done((bf16[8,1,8192]{2,0,1:T(8,128)(2,1)S(1)}, bf16[8,1,8192]{2,0,1:T(8,128)(2,1)S(1)}, u32[]{:S(2)}, u32[]{:S(2)}) %collective-permute-start.1) | collective-permute-done | bytes 131104 | tf_op jit(solution)/shard_map/ppermute | solution.py:103
  44.5 5.9 %collective-permute-done.2 = bf16[8,1,8192]{2,0,1:T(8,128)(2,1)S(1)} collective-permute-done((bf16[8,1,8192]{2,0,1:T(8,128)(2,1)S(1)}, bf16[8,1,8192]{2,0,1:T(8,128)(2,1)S(1)}, u32[]{:S(2)}, u32[]{:S(2)}) %collective-permute-start.2) | collective-permute-done | bytes 131104 | tf_op jit(solution)/shard_map/ppermute | solution.py:103
  50.4 0.8 copy-done.2
  51.3 0.6 dynamic-slice
  52.5 102.2 %all-reduce.6.cloned.1.call-done = f32[16,8192]{1,0:T(8,128)} async-done(((f32[16,8192]{1,0:T(8,128)}), f32[16,8192]{1,0:T(8,128)}) %all-reduce.6.cloned.1.call-update) | async-done | bytes 524304
  154.7 1.0 constant_dynamic-slice_fusion
  155.7 0.7 concatenate.3
  156.4 0.7 dynamic-slice.2
  157.1 41.8 %all-reduce.8.cloned.1.call-done = f32[4,8192]{1,0:T(4,128)} async-done(((f32[4,8192]{1,0:T(4,128)}), f32[4,8192]{1,0:T(4,128)}) %all-reduce.8.cloned.1.call-update) | async-done | bytes 131088
  198.9 2.3 %broadcast_select_fusion = bf16[1,1,1,8192]{3,2,1,0:T(2,128)(2,1)} fusion(pred[]{:T(512)S(6)} %lt.49, f32[4,8192]{1,0:T(4,128)} %all-reduce.8.cloned.1.call-done, u32[]{:T(128)} %bitcast.23, f32[1,1,1,8192]{3,2,1,0:T(1,128)S(1)} %bitcast.74, bf16[1,1,1,8192]{3,2,1,0:T(2,128)(2,1)S(1)} %copy-done.3), kind=kLoop, calls=%fused_computation.31 | loop fusion | flops 40960 | bytes 98309 | tf_op jit(solution)/shard_map/jit(_where)/select_n | solution.py:125
  (22 shorter events, 0.3 us)
Async XLA Ops:
  6.5 2.4 %copy-start = (bf16[1,1,1,8192]{3,2,1,0:T(2,128)(2,1)S(1)}, bf16[1,1,1,8192]{3,2,1,0:T(2,128)(2,1)}, u32[]{:S(2)}) copy-start(bf16[1,1,1,8192]{3,2,1,0:T(2,128)(2,1)} %param.16) | copy-start | bytes 49156
  6.5 148.2 %all-reduce.6.cloned.1.call-start = ((), (), s32[]{:S(2)}) async-start(), calls=%async_computation | async-start | bytes 1048576
  31.9 6.7 %collective-permute-start = (bf16[8,1,8192]{2,0,1:T(8,128)(2,1)S(1)}, bf16[8,1,8192]{2,0,1:T(8,128)(2,1)S(1)}, u32[]{:S(2)}, u32[]{:S(2)}) collective-permute-start(bf16[8,1,8192]{2,0,1:T(8,128)(2,1)S(1)} %reshape.154), channel_id=1, source_target_pairs={{0,8},{8,16},{16,24},{24,0},{1,9},{9,17},{17,25},{25,1},{2,10},{10... | collective-permute-start | bytes 393224 | tf_op jit(solution)/shard_map/ppermute | solution.py:103
  38.6 5.9 %collective-permute-start.1 = (bf16[8,1,8192]{2,0,1:T(8,128)(2,1)S(1)}, bf16[8,1,8192]{2,0,1:T(8,128)(2,1)S(1)}, u32[]{:S(2)}, u32[]{:S(2)}) collective-permute-start(bf16[8,1,8192]{2,0,1:T(8,128)(2,1)S(1)} %collective-permute-done), channel_id=1, source_target_pairs={{0,8},{8,16},{16,24},{24,0},{1,9},{9,17},{17,25},{25,1},{2,10},{10... | collective-permute-start | bytes 393224 | tf_op jit(solution)/shard_map/ppermute | solution.py:103
  44.5 5.9 %collective-permute-start.2 = (bf16[8,1,8192]{2,0,1:T(8,128)(2,1)S(1)}, bf16[8,1,8192]{2,0,1:T(8,128)(2,1)S(1)}, u32[]{:S(2)}, u32[]{:S(2)}) collective-permute-start(bf16[8,1,8192]{2,0,1:T(8,128)(2,1)S(1)} %collective-permute-done.1), channel_id=1, source_target_pairs={{0,8},{8,16},{16,24},{24,0},{1,9},{9,17},{17,25},{25,1},{2,10},{10... | collective-permute-start | bytes 393224 | tf_op jit(solution)/shard_map/ppermute | solution.py:103
  50.3 0.9 copy-start.5
  50.3 106.1 %copy-start.4 = (u32[32]{0:T(128)S(1)}, u32[32]{0:T(128)}, u32[]{:S(2)}) copy-start(u32[32]{0:T(128)} %constant.90) | copy-start | bytes 388
  50.3 148.6 %copy-start.3 = (bf16[1,1,1,8192]{3,2,1,0:T(2,128)(2,1)S(1)}, bf16[1,1,1,8192]{3,2,1,0:T(2,128)(2,1)}, u32[]{:S(2)}) copy-start(bf16[1,1,1,8192]{3,2,1,0:T(2,128)(2,1)} %param.19) | copy-start | bytes 49156
  50.4 0.8 copy-start.2
  50.4 150.8 %copy-start.1 = (bf16[1,1,1,8192]{3,2,1,0:T(2,128)(2,1)S(1)}, bf16[1,1,1,8192]{3,2,1,0:T(2,128)(2,1)}, u32[]{:S(2)}) copy-start(bf16[1,1,1,8192]{3,2,1,0:T(2,128)(2,1)} %param.16) | copy-start | bytes 49156
  51.2 147.7 %all-reduce.8.cloned.1.call-start = ((), (), s32[]{:S(2)}) async-start(), calls=%async_computation.1 | async-start | bytes 262144
Sparse Core Ops, SparseCore 0:
  51.3 103.3 all-reduce.5
  157.6 41.2 all-reduce.7
